TPU v7x, 32 devices: a whole 2x2x4 slice. The times are simulated.
32 devices in a mesh: tm: 2 (over x), src: 16 (over z, y, core).
Axes of the slice: x: 2, y: 2, z: 4, core: 2. Of those that a mesh axis runs over, the one named last changes fastest.
Arguments:
- design: float32 [16, 524288], P(None, ('tm', 'src')), may hold values from -2 to 2
- unit_index: int32 [524288], P(('tm', 'src')), may hold values from 0 to 255, as said below
- residual: float32 [524288], P(('tm', 'src')), may hold values from -6 to 6
- weight: float32 [524288], P(('tm', 'src')), may hold values from 0.25 to 4
- obs_count: int32 [32], P(('tm', 'src')), may hold values from 1 to 16384, as said below
- damping: float32 [256], P(('tm', 'src')), may hold values from 1 to 10
Outputs:
- solution: float32 [16, 256], P(None, ('tm', 'src'))
- misfit: float32 [], replicated
Inputs may be any that keep to these rules, and one draw needn't show every extreme that they name: `unit_index`: an observation on a device of tm index g names a unit in [g * 128, (g + 1) * 128). `obs_count`: some device has all 16384 slots live.
All inputs are finite; a program needn't handle non-finite values.
Results may differ from a plain program's by a relative error of at most 0.0003.
Values sent between devices are 32-bit elements; how exact they have to be, the bound alone decides.
No kernel may reach another device: no remote copies, remote signals or barrier semaphores. Data moves between devices by JAX's collectives and lax.ppermute only.
A program may use at most 64 MiB of HBM per device.

v0:
```python
import jax
import jax.numpy as jnp
from jax import lax
from jax.sharding import PartitionSpec as P


def make_reader(stacked):

    def reader(row, column):
        return stacked[row * 16 + column]

    return reader


def block_solve(reader, rhs, damping):
    lower = {}
    for j in range(16):
        running = reader(j, j) + damping
        for k in range(j):
            running = running - lower[j, k] * lower[j, k]
        diag_term = jnp.sqrt(running)
        lower[j, j] = diag_term
        for i in range(j + 1, 16):
            running = reader(i, j)
            for k in range(j):
                running = running - lower[i, k] * lower[j, k]
            lower[i, j] = running / diag_term
    forward = []
    for i in range(16):
        running = rhs[i]
        for k in range(i):
            running = running - lower[i, k] * forward[k]
        forward.append(running / lower[i, i])
    backward = [None] * 16
    for i in range(15, -1, -1):
        running = forward[i]
        for k in range(i + 1, 16):
            running = running - lower[k, i] * backward[k]
        backward[i] = running / lower[i, i]
    return jnp.stack(backward)


def quadratic_terms(reader, rhs, solution_own):
    quadratic = jnp.zeros((), jnp.float32)
    for i in range(16):
        applied = jnp.zeros_like(solution_own[0])
        for j in range(16):
            applied = applied + reader(max(i, j), min(i, j)) * solution_own[j]
        quadratic = quadratic + jnp.sum(solution_own[i] * applied)
    return quadratic - 2.0 * jnp.sum(solution_own * rhs)


def on_device(design, unit_index, residual, weight, obs_count, damping):
    n_source = lax.axis_size("src")
    own_units = damping.shape[0]
    units_group = own_units * n_source
    slots = design.shape[1]
    local_unit = unit_index - lax.axis_index("tm") * units_group
    weights_on = jnp.where(
        jnp.arange(slots, dtype=jnp.int32) < obs_count[0], weight, jnp.zeros_like(weight)
    )
    block_rows = 1024
    turns = slots // block_rows
    pair_count = 256

    def pair_rows(rows):
        return (rows[:, None, :] * rows[None, :, :]).reshape(256, rows.shape[1])

    unit_range = jnp.arange(units_group, dtype=jnp.int32)

    def accumulate(step, partial_value):
        begin = step * block_rows
        rows = lax.dynamic_slice_in_dim(design, begin, block_rows, 1)
        units_of = lax.dynamic_slice_in_dim(local_unit, begin, block_rows, 0)
        resid = lax.dynamic_slice_in_dim(residual, begin, block_rows, 0)
        weights_blk = lax.dynamic_slice_in_dim(weights_on, begin, block_rows, 0)
        stacked = jnp.concatenate(
            [pair_rows(rows) * weights_blk, rows * (weights_blk * resid)], axis=0
        )
        one_hot = (units_of[:, None] == unit_range[None, :]).astype(jnp.float32)
        return partial_value + jnp.dot(
            stacked, one_hot, precision=lax.Precision.HIGHEST, preferred_element_type=jnp.float32
        )

    start = jnp.zeros((pair_count + 16, units_group), jnp.float32)
    partial_value = lax.fori_loop(0, turns, accumulate, start)
    own_part = lax.psum_scatter(partial_value, "src", scatter_dimension=1, tiled=True)
    solution_own = block_solve(make_reader(own_part), own_part[pair_count:], damping)
    unit_terms = quadratic_terms(make_reader(own_part), own_part[pair_count:], solution_own)
    before = jnp.sum(weights_on * residual * residual)
    chi_total, weight_total = lax.psum((before + unit_terms, jnp.sum(weights_on)), ("tm", "src"))
    return (solution_own, chi_total / weight_total)


def solution(mesh):
    placed = (
        P(None, ("tm", "src")),
        P(("tm", "src")),
        P(("tm", "src")),
        P(("tm", "src")),
        P(("tm", "src")),
        P(("tm", "src")),
    )
    return jax.shard_map(
        on_device,
        mesh=mesh,
        in_specs=placed,
        out_specs=(P(None, ("tm", "src")), P()),
        check_vma=False,
    )
```

profile of v0, /device:TPU:0, one launch (start us, length us, event | category | flops | bytes accessed | tf_op | source)
XLA Modules:
  0.0 241.2 jit_solution(16647316104159535777)
XLA Ops:
  7.9 0.8 broadcast_subtract_fusion
  8.7 1.6 fusion.56
  10.3 42.7 %while.14 = (s32[]{:T(128)}, f32[272,128]{1,0:T(8,128)S(1)}, f32[16,16384]{1,0:T(8,128)}, f32[16384]{0:T(1024)S(1)}, f32[16384]{0:T(1024)}, /*index=5*/s32[16384...) while((s32[]{:T(128)}, f32[272,128]{1,0:T(8,128)S(1)}, f32[16,16384]{1,0:T(8,128)}, ...), condition=%wide.region_1.2_spmd.clone, body=%wide.region_0.1_spmd.clone.sunk | while | flops 428839936 | bytes 4837545 | solution.py:86
  11.0 0.8 broadcast_multiply_fusion.4
  12.1 0.8 convolution_add_fusion.2
  13.7 0.8 broadcast_multiply_fusion.4
  16.3 0.8 broadcast_multiply_fusion.4
  17.5 0.8 convolution_add_fusion.2
  19.0 0.8 broadcast_multiply_fusion.4
  20.1 0.8 convolution_add_fusion.2
  21.7 0.8 broadcast_multiply_fusion.4
  22.8 0.8 convolution_add_fusion.2
  24.4 0.8 broadcast_multiply_fusion.4
  27.0 0.8 broadcast_multiply_fusion.4
  29.7 0.8 broadcast_multiply_fusion.4
  32.4 0.8 broadcast_multiply_fusion.4
  33.5 0.8 convolution_add_fusion.2
  35.0 0.8 broadcast_multiply_fusion.4
  37.7 0.8 broadcast_multiply_fusion.4
  40.4 0.8 broadcast_multiply_fusion.4
  43.0 0.8 broadcast_multiply_fusion.4
  45.7 0.8 broadcast_multiply_fusion.4
  46.8 0.8 convolution_add_fusion.2
  48.4 0.8 broadcast_multiply_fusion.4
  51.0 0.8 broadcast_multiply_fusion.4
  54.9 90.6 %all-reduce.4.cloned.1.call-done = f32[272,128]{1,0:T(8,128)} async-done(((f32[272,128]{1,0:T(8,128)}), f32[272,128]{1,0:T(8,128)}) %all-reduce.4.cloned.1.call-update) | async-done | bytes 139280
  145.5 1.0 subtract_divide_fusion.110
  146.4 1.2 subtract_sqrt_fusion.8
  147.7 2.8 %subtract_divide_fusion.29 = (f32[8]{0:T(128)S(1)}, f32[8]{0:T(128)S(1)}, f32[8]{0:T(128)S(1)}, f32[8]{0:T(128)S(1)}, f32[8]{0:T(128)S(1)}, /*index=5*/f32[8]{0:...) fusion(f32[272,128]{1,0:T(8,128)} %all-reduce.4.cloned.1.call-d, ...), kind=kLoop, calls=%fused_computation.264 | loop fusion | flops 10472 | bytes 10624 | tf_op jit(solution)/shard_map/div | solution.py:33
  150.5 1.5 subtract_divide_fusion.15
  152.0 1.9 multiply_reduce_fusion
  154.6 1.4 fusion.9
  156.8 1.5 multiply_reduce_fusion.14
  158.2 1.4 multiply_reduce_fusion.15
  161.0 1.5 multiply_reduce_fusion.13
  163.2 1.5 multiply_reduce_fusion.12
  165.3 1.5 multiply_reduce_fusion.11
  167.5 1.5 multiply_reduce_fusion.10
  169.7 1.5 multiply_reduce_fusion.9
  171.8 1.5 multiply_reduce_fusion.8
  174.0 1.5 multiply_reduce_fusion.7
  176.2 1.5 multiply_reduce_fusion.6
  178.3 1.5 multiply_reduce_fusion.5
  180.5 1.5 multiply_reduce_fusion.4
  182.7 1.5 multiply_reduce_fusion.3
  184.8 1.5 multiply_reduce_fusion.2
  187.0 1.5 multiply_reduce_fusion.1
  190.5 41.3 %all-reduce.1 = (f32[]{:T(128)}, f32[]{:T(128)}) all-reduce(f32[]{:T(128)S(6)} %add.1126, f32[]{:T(128)} %get-tuple-element.154), channel_id=1, replica_groups=mesh['tm'=2,'src'=16] {'tm','src'}, use_global_device_ids=true, to_apply=%region_21.22 | all-reduce | flops 2 | bytes 16 | tf_op jit(solution)/shard_map/psum | solution.py:91
  (86 shorter events, 25.3 us)
Async XLA Ops:
  7.2 138.3 %all-reduce.4.cloned.1.call-start = ((), (), s32[]{:S(2)}) async-start(), calls=%async_computation | async-start | bytes 278528
  10.3 43.4 %copy-start.2 = (u32[32]{0:T(128)S(1)}, u32[32]{0:T(128)}, u32[]{:S(2)}) copy-start(u32[32]{0:T(128)} %constant.48) | copy-start | bytes 388
  10.3 135.2 %copy-start.1 = (f32[8]{0:T(128)S(1)}, f32[8]{0:T(128)}, u32[]{:S(2)}) copy-start(f32[8]{0:T(128)} %param.13) | copy-start | bytes 100
  53.0 0.7 copy-start
Sparse Core Ops, SparseCore 0:
  53.8 91.6 all-reduce.3
where the time goes:
time: 244 us; the launch traced here: 241 us
  waiting for transfers between devices  90.6 us (37%)
  other arithmetic  62.9 us (26%)
  blocking collectives  41.3 us (17%)
  between operations  30.2 us (12%)
  matrix products  13.1 us (5%)
    unnamed x2, waiting for transfers between devices  90.6 us
    psum x1, blocking collectives, on_device(): lax.psum((before + unit_terms, jnp.sum(weights_on)), ('tm', 'src'))  41.3 us
    reduce_sum x16, other arithmetic, quadratic_terms(): quadratic = quadratic + jnp.sum(solution_own[i] * applied)  24 us
    mul x16, other arithmetic, accumulate(): rows * (weights_blk * resid)  13.6 us
    dot_general x16, matrix products, accumulate(): jnp.dot(stacked, one_hot, precision=lax.Precision.HIGHEST, preferred_elem...  13.1 us
    mul x16, other arithmetic, accumulate(): weights_blk * resid  11.1 us
  transfers between devices with their start and end apart: 1, of which 1 were waited for; matrix products, arithmetic and copies ran while one was open for 0% of the time, Pallas kernels for 0%

commit v1 on v0

v1 whole, which is shorter than its diff:
```python
import jax
import jax.numpy as jnp
from jax import lax
from jax.experimental import pallas as pl
from jax.experimental.pallas import tpu as pltpu
from jax.sharding import PartitionSpec as P

HIGHER = 5
CROSS = 8
ROWS = 160
ROW_WEIGHT, ROW_BEFORE, ROW_DAMPING = 36, 37, 38
CHUNK = 4096
PIECE = 1024


def row_of(i, j):
    if i < 8 or j >= 8:
        base = 0 if i < 8 else 40
        a, b = i % 8, j % 8
        s = a - b
        return base + (s * 8 + b if s <= 4 else (8 - s) * 8 + a)
    return 80 + ((i - 8 - j) % 8) * 8 + j


def accumulate_kernel(count_ref, design_ref, unit_ref, resid_ref, weight_ref, damping_ref, keep_ref, send_ref, acc_ref, side_ref):
    step = pl.program_id(0)
    chunk = design_ref.shape[1]
    units = acc_ref.shape[1]
    piece = min(PIECE, chunk)
    src = lax.axis_index("src")
    first_unit = lax.axis_index("tm") * units
    count = count_ref[0]

    @pl.when(step == 0)
    def _():
        acc_ref[...] = jnp.zeros_like(acc_ref)
        side_ref[...] = jnp.zeros_like(side_ref)

    unit_rows = lax.broadcasted_iota(jnp.int32, (units, piece), 0)
    slot = lax.broadcasted_iota(jnp.int32, (1, piece), 1) + step * chunk
    total = jnp.zeros((2 * ROWS, units), jnp.float32)
    weight_sum = jnp.zeros((1, 128), jnp.float32)
    before_sum = jnp.zeros((1, 128), jnp.float32)
    for begin in range(0, chunk, piece):
        at = pl.ds(begin, piece)
        rows = design_ref[:, at]
        resid = resid_ref[:, at]
        weight = jnp.where(slot + begin < count, weight_ref[:, at], 0.0)
        first, second = rows[:8], rows[8:]
        wfirst, wsecond = first * weight, second * weight
        groups = [wfirst * (pltpu.roll(first, 8 - s, 0) if s else first) for s in range(HIGHER)]
        turned = [pltpu.roll(second, 8 - s, 0) if s else second for s in range(CROSS)]
        groups += [wsecond * turned[s] for s in range(HIGHER)]
        groups += [wfirst * turned[s] for s in range(CROSS)]
        groups += [wfirst * resid, wsecond * resid]
        high, low = [], []
        for a, b in zip(groups[::2], groups[1::2]):
            both = jnp.concatenate([a, b], axis=0)
            top = both.astype(jnp.bfloat16)
            high.append(top)
            low.append((both - top.astype(jnp.float32)).astype(jnp.bfloat16))
        stacked = jnp.concatenate(high + low, axis=0)
        local = unit_ref[:, at] - first_unit
        one_hot = jnp.where(unit_rows == local, 1.0, 0.0).astype(jnp.bfloat16)
        total = total + lax.dot_general(stacked, one_hot, (((1,), (1,)), ((), ())), preferred_element_type=jnp.float32)
        before = weight * resid * resid
        for k in range(0, piece, 128):
            weight_sum = weight_sum + weight[:, k:k + 128]
            before_sum = before_sum + before[:, k:k + 128]
    acc_ref[...] += total[:ROWS] + total[ROWS:]
    side_ref[0:1] += weight_sum
    side_ref[1:2] += before_sum

    @pl.when(step == pl.num_programs(0) - 1)
    def _():
        acc_ref[ROW_WEIGHT:ROW_DAMPING + 1, :] = jnp.zeros((3, units), jnp.float32)
        acc_ref[ROW_WEIGHT:ROW_BEFORE + 1, 0:128] = side_ref[0:2]
        own = damping_ref.shape[1]
        padded = jnp.concatenate([damping_ref[...], jnp.zeros((1, units - own), jnp.float32)], axis=1)
        placed = pltpu.roll(jnp.broadcast_to(padded, (8, units)), src * own, 1)
        acc_ref[ROW_DAMPING:ROW_DAMPING + 1, :] = placed[0:1]
        half = ROWS // 2
        bit = src % 2
        keep_ref[...] = acc_ref[pl.ds(pl.multiple_of(bit * half, 8), half), :]
        send_ref[...] = acc_ref[pl.ds(pl.multiple_of((1 - bit) * half, 8), half), :]


def solve_kernel(mine_ref, other_ref, solution_ref, stats_ref, full_ref, column_ref):
    units = mine_ref.shape[1]
    own = solution_ref.shape[1]
    src = lax.axis_index("src")
    half = ROWS // 2
    bit = src % 2
    full_ref[pl.ds(pl.multiple_of(bit * half, 8), half), :] = mine_ref[...]
    full_ref[pl.ds(pl.multiple_of((1 - bit) * half, 8), half), :] = other_ref[...]
    column_ref[...] = jnp.zeros_like(column_ref)
    for j in range(16):
        for i in range(j, 16):
            r = row_of(i, j)
            column_ref[j * 24 + i:j * 24 + i + 1, :] = full_ref[r:r + 1, :]
        column_ref[j * 24 + 16:j * 24 + 17, :] = full_ref[144 + j:145 + j, :]
    damping = full_ref[ROW_DAMPING:ROW_DAMPING + 1, :]
    upper = [column_ref[j * 24:j * 24 + 8, :] for j in range(8)]
    lower = [column_ref[j * 24 + 8:j * 24 + 24, :] for j in range(16)]

    def entry(top, bottom, i):
        return top[i:i + 1] if i < 8 else bottom[i - 8:i - 7]

    inverse, forward = [], []
    for j in range(16):
        inv = lax.rsqrt(entry(upper[j] if j < 8 else None, lower[j], j) + damping)
        inverse.append(inv)
        if j < 8:
            upper[j] = upper[j] * inv
        lower[j] = lower[j] * inv
        forward.append(lower[j][8:9])
        for k in range(j + 1, 16):
            factor = entry(upper[j] if j < 8 else None, lower[j], k)
            lower[k] = lower[k] - lower[j] * factor
            if k < 8:
                upper[k] = upper[k] - upper[j] * factor
    sub = lax.broadcasted_iota(jnp.int32, (8, units), 0)
    low_x = jnp.zeros((8, units), jnp.float32)
    high_x = jnp.zeros((8, units), jnp.float32)
    for i in range(15, -1, -1):
        part = lower[i][:8] * high_x
        if i < 8:
            part = part + upper[i] * low_x
        x = (forward[i] - jnp.sum(part, axis=0, keepdims=True)) * inverse[i]
        if i < 8:
            low_x = jnp.where(sub == i, x, low_x)
        else:
            high_x = jnp.where(sub == i - 8, x, high_x)
    squares = damping * jnp.sum(low_x * low_x + high_x * high_x, axis=0, keepdims=True)
    for y in forward:
        squares = squares + y * y
    chi = jnp.sum(full_ref[ROW_BEFORE:ROW_BEFORE + 1, :] - squares, axis=1, keepdims=True)
    weight = jnp.sum(full_ref[ROW_WEIGHT:ROW_WEIGHT + 1, :], axis=1, keepdims=True)
    stats_ref[...] = jnp.where(lax.broadcasted_iota(jnp.int32, (8, 128), 0) == 0, chi, weight)
    shift = (units - src * own) % units
    solution_ref[0:8, :] = pltpu.roll(low_x, shift, 1)[:, :own]
    solution_ref[8:16, :] = pltpu.roll(high_x, shift, 1)[:, :own]


def swap(x, axis, mask):
    size = lax.axis_size(axis)
    return lax.ppermute(x, axis, [(k, k ^ mask) for k in range(size)])


def masks_of(size):
    masks = []
    b = 1
    while (1 << b) < size:
        masks.append((1 << b) if b < 3 else (1 << b) | (1 << (b - 1)))
        b += 1
    return masks


def on_device(design, unit_index, residual, weight, obs_count, damping):
    n_source = lax.axis_size("src")
    own_units = damping.shape[0]
    units = own_units * n_source
    slots = design.shape[1]
    chunk = min(CHUNK, slots)
    half = ROWS // 2
    line = lambda: pl.BlockSpec((1, chunk), lambda s: (0, s))
    keep, send = pl.pallas_call(
        accumulate_kernel,
        grid=(slots // chunk,),
        in_specs=[
            pl.BlockSpec(memory_space=pltpu.SMEM),
            pl.BlockSpec((16, chunk), lambda s: (0, s)),
            line(), line(), line(),
            pl.BlockSpec((1, own_units), lambda s: (0, 0)),
        ],
        out_specs=[pl.BlockSpec((half, units), lambda s: (0, 0))] * 2,
        out_shape=[jax.ShapeDtypeStruct((half, units), jnp.float32)] * 2,
        scratch_shapes=[pltpu.VMEM((ROWS, units), jnp.float32), pltpu.VMEM((8, 128), jnp.float32)],
        compiler_params=pltpu.CompilerParams(dimension_semantics=("arbitrary",)),
        name="accumulate",
    )(obs_count, design, unit_index.reshape(1, slots), residual.reshape(1, slots), weight.reshape(1, slots), damping.reshape(1, own_units))
    mine = keep + swap(send, "src", 1)
    for mask in masks_of(n_source):
        mine = mine + swap(mine, "src", mask)
    other = swap(mine, "src", 1)
    solution_own, stats = pl.pallas_call(
        solve_kernel,
        out_shape=[jax.ShapeDtypeStruct((16, own_units), jnp.float32), jax.ShapeDtypeStruct((8, 128), jnp.float32)],
        scratch_shapes=[pltpu.VMEM((ROWS, units), jnp.float32), pltpu.VMEM((16 * 24, units), jnp.float32)],
        name="solve",
    )(mine, other)
    n_time = lax.axis_size("tm")
    mask = 1
    while mask < n_time:
        stats = stats + swap(stats, "tm", mask)
        mask *= 2
    return (solution_own, stats[0, 0] / stats[1, 0])


def solution(mesh):
    placed = (
        P(None, ("tm", "src")),
        P(("tm", "src")),
        P(("tm", "src")),
        P(("tm", "src")),
        P(("tm", "src")),
        P(("tm", "src")),
    )
    return jax.shard_map(
        on_device,
        mesh=mesh,
        in_specs=placed,
        out_specs=(P(None, ("tm", "src")), P()),
        check_vma=False,
    )
```

time: 244 us -> 35.1 us (0.14); the launches traced: 241 us -> 34.7 us
  waiting for transfers between devices: 90.6 us -> 8.98 us
  other arithmetic: 62.9 us -> 0.81 us
  blocking collectives: 41.3 us -> 0 us
  between operations: 30.2 us -> 3.74 us
  matrix products: 13.1 us -> 0 us
  starting transfers between devices: 0.04 us -> 11.3 us
  Pallas kernels: 0 us -> 7.38 us
    unnamed x2 -> x0, waiting for transfers between devices: 90.6 us -> none
    psum x1 -> x0, blocking collectives: 41.3 us -> none  [on_device(): lax.psum((before + unit_terms, jnp.sum(weights_on)), ('tm', 'src'))]
    mul x64 -> x0, other arithmetic: 28.5 us -> none  [the longest x16 13.6 us: accumulate(): rows * (weights_blk * resid)]
    reduce_sum x18 -> x0, other arithmetic: 27.1 us -> none  [the longest x16 24 us: quadratic_terms(): quadratic = quadratic + jnp.sum(solution_own[i] * applied)]
    dot_general x16 -> x0, matrix products: 13.1 us -> none  [accumulate(): jnp.dot(stacked, one_hot, precision=lax.Precision.HIGHEST, preferred_elem...]
    ppermute x0 -> x6, starting transfers between devices: none -> 11.3 us  [swap(): return lax.ppermute(x, axis, [(k, k ^ mask) for k in range(size)])]
    ppermute x0 -> x6, waiting for transfers between devices: none -> 8.98 us  [swap(): return lax.ppermute(x, axis, [(k, k ^ mask) for k in range(size)])]
    pallas_call x0 -> x2, Pallas kernels: none -> 7.38 us  [the longest x1 5.43 us: on_device(): pl.pallas_call(accumulate_kernel, grid=(slots // chunk,), in_specs=[pl.Bl...]
  transfers between devices with their start and end apart: 1 -> 6, of which waited for: 1 -> 6; matrix products, arithmetic and copies ran while one was open for 0% -> 4% of each run, Pallas kernels for 0% -> 0%
where the time goes in v1:
time: 35.1 us; the launch traced here: 34.7 us
  starting transfers between devices  11.3 us (32%)
  waiting for transfers between devices  8.98 us (26%)
  Pallas kernels  7.38 us (21%)
  between operations  3.74 us (11%)
  local copies, waits for them, and re-layouts  2.56 us (7%)
  other arithmetic  0.81 us (2%)
    ppermute x6, starting transfers between devices, swap(): return lax.ppermute(x, axis, [(k, k ^ mask) for k in range(size)])  11.3 us
    ppermute x6, waiting for transfers between devices, swap(): return lax.ppermute(x, axis, [(k, k ^ mask) for k in range(size)])  8.98 us
    pallas_call x1, Pallas kernels, on_device(): pl.pallas_call(accumulate_kernel, grid=(slots // chunk,), in_specs=[pl.Bl...  5.43 us
    unnamed x7, local copies, waits for them, and re-layouts  1.98 us
    pallas_call x1, Pallas kernels, on_device(): pl.pallas_call(solve_kernel, out_shape=[jax.ShapeDtypeStruct((16, own_uni...  1.95 us
    add x1, other arithmetic, on_device(): mine = keep + swap(send, 'src', 1)  0.78 us
  transfers between devices with their start and end apart: 6, of which 6 were waited for; matrix products, arithmetic and copies ran while one was open for 4% of the time, Pallas kernels for 0%

profile of v1, /device:TPU:0, one launch (start us, length us, event | category | flops | bytes accessed | tf_op | source)
XLA Modules:
  0.0 34.7 jit_solution(433545035637764300)
XLA Ops:
  1.3 5.4 %accumulate.1 = (f32[80,128]{1,0:T(8,128)}, f32[80,128]{1,0:T(8,128)}) custom-call(s32[1]{0:T(128)S(6)} %copy.9.count_ref, f32[16,16384]{1,0:T(8,128)} %design_ref.1, s32[1,16384]{1,0:T(1,128)} %bitcast.5, f32[1,16384]{1,0:T(1,128)} %bitcast.6, f32[1,16384]{1,0:T(1,128)} %bitcast.7, f32[1,8]{1,0:T(1,128)} %bitcast.8), custom_call_target="tpu_custom_call" | custom-call | tf_op jit(solution)/shard_map/accumulate/pallas_call | solution.py:167
  6.7 0.5 %collective-permute-start = (f32[80,128]{1,0:T(8,128)}, f32[80,128]{1,0:T(8,128)S(1)}, u32[]{:S(2)}, u32[]{:S(2)}) collective-permute-start(f32[80,128]{1,0:T(8,128)} %get-tuple-element.7), channel_id=1, source_target_pairs={{0,1},{1,0},{2,3},{3,2},{4,5},{5,4},{6,7},{7,6},{8,9},{9,8},{10,11... | collective-permute-start | bytes 122888 | tf_op jit(solution)/shard_map/ppermute | solution.py:147
  7.2 1.1 %collective-permute-done = f32[80,128]{1,0:T(8,128)S(1)} collective-permute-done((f32[80,128]{1,0:T(8,128)}, f32[80,128]{1,0:T(8,128)S(1)}, u32[]{:S(2)}, u32[]{:S(2)}) %collective-permute-start) | collective-permute-done | bytes 40992 | tf_op jit(solution)/shard_map/ppermute | solution.py:147
  8.3 0.8 %add.15 = f32[80,128]{1,0:T(8,128)S(1)} add(f32[80,128]{1,0:T(8,128)} %get-tuple-element.6, f32[80,128]{1,0:T(8,128)S(1)} %collective-permute-done) | non-fusion elementwise | flops 10240 | bytes 122880 | tf_op jit(solution)/shard_map/add | solution.py:182
  9.1 2.8 %collective-permute-start.1 = (f32[80,128]{1,0:T(8,128)S(1)}, f32[80,128]{1,0:T(8,128)S(1)}, u32[]{:S(2)}, u32[]{:S(2)}) collective-permute-start(f32[80,128]{1,0:T(8,128)S(1)} %add.15), channel_id=1, source_target_pairs={{0,2},{1,3},{2,0},{3,1},{4,6},{5,7},{6,4},{7,5},{8,10},{9,11},{10,... | collective-permute-start | bytes 122888 | tf_op jit(solution)/shard_map/ppermute | solution.py:147
  11.9 2.0 %collective-permute-done.1 = f32[80,128]{1,0:T(8,128)S(1)} collective-permute-done((f32[80,128]{1,0:T(8,128)S(1)}, f32[80,128]{1,0:T(8,128)S(1)}, u32[]{:S(2)}, u32[]{:S(2)}) %collective-permute-start.1) | collective-permute-done | bytes 40992 | tf_op jit(solution)/shard_map/ppermute | solution.py:147
  13.9 2.1 %collective-permute-start.2 = (f32[80,128]{1,0:T(8,128)S(1)}, f32[80,128]{1,0:T(8,128)S(1)}, u32[]{:S(2)}, u32[]{:S(2)}) collective-permute-start(f32[80,128]{1,0:T(8,128)S(1)} %add.16), channel_id=1, source_target_pairs={{0,4},{1,5},{2,6},{3,7},{4,0},{5,1},{6,2},{7,3},{8,12},{9,13},{10,... | collective-permute-start | bytes 122888 | tf_op jit(solution)/shard_map/ppermute | solution.py:147
  16.0 2.0 %collective-permute-done.2 = f32[80,128]{1,0:T(8,128)S(1)} collective-permute-done((f32[80,128]{1,0:T(8,128)S(1)}, f32[80,128]{1,0:T(8,128)S(1)}, u32[]{:S(2)}, u32[]{:S(2)}) %collective-permute-start.2) | collective-permute-done | bytes 40992 | tf_op jit(solution)/shard_map/ppermute | solution.py:147
  18.0 4.1 %collective-permute-start.3 = (f32[80,128]{1,0:T(8,128)S(1)}, f32[80,128]{1,0:T(8,128)S(1)}, u32[]{:S(2)}, u32[]{:S(2)}) collective-permute-start(f32[80,128]{1,0:T(8,128)S(1)} %add.17), channel_id=1, source_target_pairs={{0,12},{1,13},{2,14},{3,15},{4,8},{5,9},{6,10},{7,11},{8,4},{9,5},... | collective-permute-start | bytes 122888 | tf_op jit(solution)/shard_map/ppermute | solution.py:147
  22.0 2.0 %collective-permute-done.3 = f32[80,128]{1,0:T(8,128)S(1)} collective-permute-done((f32[80,128]{1,0:T(8,128)S(1)}, f32[80,128]{1,0:T(8,128)S(1)}, u32[]{:S(2)}, u32[]{:S(2)}) %collective-permute-start.3) | collective-permute-done | bytes 40992 | tf_op jit(solution)/shard_map/ppermute | solution.py:147
  24.0 0.0 copy-start
  24.0 0.1 collective-permute-start.4
  24.1 1.2 %collective-permute-done.4.other_ref = f32[80,128]{1,0:T(8,128)S(1)} collective-permute-done((f32[80,128]{1,0:T(8,128)S(1)}, f32[80,128]{1,0:T(8,128)S(1)}, u32[]{:S(2)}, u32[]{:S(2)}) %collective-permute-start.4) | collective-permute-done | bytes 40992 | tf_op jit(solution)/shard_map/ppermute | solution.py:147
  25.3 0.0 copy-done
  25.3 0.0 copy-start.1
  25.3 0.6 %copy-done.1 = f32[80,128]{1,0:T(8,128)} copy-done((f32[80,128]{1,0:T(8,128)}, f32[80,128]{1,0:T(8,128)S(1)}, u32[]{:S(2)}) %copy-start.1) | copy-done | bytes 40984
  25.9 1.9 %solve.1 = (f32[16,8]{1,0:T(8,128)}, f32[8,128]{1,0:T(8,128)}) custom-call(f32[80,128]{1,0:T(8,128)} %copy-done, f32[80,128]{1,0:T(8,128)} %copy-done.1), custom_call_target="tpu_custom_call" | custom-call | tf_op jit(solution)/shard_map/solve/pallas_call | solution.py:186
  27.9 1.7 %collective-permute-start.5 = (f32[8,128]{1,0:T(8,128)}, f32[8,128]{1,0:T(8,128)S(1)}, u32[]{:S(2)}, u32[]{:S(2)}) collective-permute-start(f32[8,128]{1,0:T(8,128)} %get-tuple-element.9), channel_id=1, source_target_pairs={{0,16},{16,0},{1,17},{17,1},{2,18},{18,2},{3,19},{19,3},{4,20},{20... | collective-permute-start | bytes 12296 | tf_op jit(solution)/shard_map/ppermute | solution.py:147
  29.6 0.0 copy-start.2
  29.6 1.4 %copy.8 = f32[16,8]{0,1:T(8,128)} copy(f32[16,8]{1,0:T(8,128)} %get-tuple-element.10) | data formatting | bytes 1024
  30.9 0.8 %collective-permute-done.5 = f32[8,128]{1,0:T(8,128)S(1)} collective-permute-done((f32[8,128]{1,0:T(8,128)}, f32[8,128]{1,0:T(8,128)S(1)}, u32[]{:S(2)}, u32[]{:S(2)}) %collective-permute-start.5) | collective-permute-done | bytes 4128 | tf_op jit(solution)/shard_map/ppermute | solution.py:147
  31.7 0.0 copy-done.2
  31.7 0.6 %fusion = (f32[1,1]{1,0:T(1,128)}, f32[1,1]{1,0:T(1,128)}) fusion(f32[8,128]{1,0:T(8,128)S(1)} %add.19), kind=kLoop, calls=%fused_computation | loop fusion | bytes 16 | tf_op jit(solution)/shard_map/slice | solution.py:197
  (4 shorter events, 0.0 us)
Async XLA Ops:
  6.7 1.6 %collective-permute-start = (f32[80,128]{1,0:T(8,128)}, f32[80,128]{1,0:T(8,128)S(1)}, u32[]{:S(2)}, u32[]{:S(2)}) collective-permute-start(f32[80,128]{1,0:T(8,128)} %get-tuple-element.7), channel_id=1, source_target_pairs={{0,1},{1,0},{2,3},{3,2},{4,5},{5,4},{6,7},{7,6},{8,9},{9,8},{10,11... | collective-permute-start | bytes 122888 | tf_op jit(solution)/shard_map/ppermute | solution.py:147
  9.1 4.8 %collective-permute-start.1 = (f32[80,128]{1,0:T(8,128)S(1)}, f32[80,128]{1,0:T(8,128)S(1)}, u32[]{:S(2)}, u32[]{:S(2)}) collective-permute-start(f32[80,128]{1,0:T(8,128)S(1)} %add.15), channel_id=1, source_target_pairs={{0,2},{1,3},{2,0},{3,1},{4,6},{5,7},{6,4},{7,5},{8,10},{9,11},{10,... | collective-permute-start | bytes 122888 | tf_op jit(solution)/shard_map/ppermute | solution.py:147
  13.9 4.1 %collective-permute-start.2 = (f32[80,128]{1,0:T(8,128)S(1)}, f32[80,128]{1,0:T(8,128)S(1)}, u32[]{:S(2)}, u32[]{:S(2)}) collective-permute-start(f32[80,128]{1,0:T(8,128)S(1)} %add.16), channel_id=1, source_target_pairs={{0,4},{1,5},{2,6},{3,7},{4,0},{5,1},{6,2},{7,3},{8,12},{9,13},{10,... | collective-permute-start | bytes 122888 | tf_op jit(solution)/shard_map/ppermute | solution.py:147
  18.0 6.0 %collective-permute-start.3 = (f32[80,128]{1,0:T(8,128)S(1)}, f32[80,128]{1,0:T(8,128)S(1)}, u32[]{:S(2)}, u32[]{:S(2)}) collective-permute-start(f32[80,128]{1,0:T(8,128)S(1)} %add.17), channel_id=1, source_target_pairs={{0,12},{1,13},{2,14},{3,15},{4,8},{5,9},{6,10},{7,11},{8,4},{9,5},... | collective-permute-start | bytes 122888 | tf_op jit(solution)/shard_map/ppermute | solution.py:147
  24.0 1.3 %copy-start = (f32[80,128]{1,0:T(8,128)}, f32[80,128]{1,0:T(8,128)S(1)}, u32[]{:S(2)}) copy-start(f32[80,128]{1,0:T(8,128)S(1)} %add.18.mine_ref) | copy-start | bytes 122884
  24.0 1.3 %collective-permute-start.4 = (f32[80,128]{1,0:T(8,128)S(1)}, f32[80,128]{1,0:T(8,128)S(1)}, u32[]{:S(2)}, u32[]{:S(2)}) collective-permute-start(f32[80,128]{1,0:T(8,128)S(1)} %add.18.mine_ref), channel_id=1, source_target_pairs={{0,1},{1,0},{2,3},{3,2},{4,5},{5,4},{6,7},{7,6},{8,9},{9,8},{10,11... | collective-permute-start | bytes 122888 | tf_op jit(solution)/shard_map/ppermute | solution.py:147
  25.3 0.6 %copy-start.1 = (f32[80,128]{1,0:T(8,128)}, f32[80,128]{1,0:T(8,128)S(1)}, u32[]{:S(2)}) copy-start(f32[80,128]{1,0:T(8,128)S(1)} %collective-permute-done.4.other_ref) | copy-start | bytes 122884
  27.9 3.8 %collective-permute-start.5 = (f32[8,128]{1,0:T(8,128)}, f32[8,128]{1,0:T(8,128)S(1)}, u32[]{:S(2)}, u32[]{:S(2)}) collective-permute-start(f32[8,128]{1,0:T(8,128)} %get-tuple-element.9), channel_id=1, source_target_pairs={{0,16},{16,0},{1,17},{17,1},{2,18},{18,2},{3,19},{19,3},{4,20},{20... | collective-permute-start | bytes 12296 | tf_op jit(solution)/shard_map/ppermute | solution.py:147
  29.6 2.1 %copy-start.2 = (f32[8,128]{1,0:T(8,128)S(1)}, f32[8,128]{1,0:T(8,128)}, u32[]{:S(2)}) copy-start(f32[8,128]{1,0:T(8,128)} %get-tuple-element.9) | copy-start | bytes 12292

commit v2 on v1

--- a/solution.py
+++ b/solution.py
@@ -9,8 +9,8 @@
 CROSS = 8
 ROWS = 160
 ROW_WEIGHT, ROW_BEFORE, ROW_DAMPING = 36, 37, 38
-CHUNK = 4096
-PIECE = 1024
+CHUNK = 8192
+PIECE = 2048
 
 
 def row_of(i, j):
@@ -29,7 +29,7 @@
     piece = min(PIECE, chunk)
     src = lax.axis_index("src")
     first_unit = lax.axis_index("tm") * units
-    count = count_ref[0]
+    count = count_ref[...]
 
     @pl.when(step == 0)
     def _():
@@ -87,7 +87,7 @@
 
 def solve_kernel(mine_ref, other_ref, solution_ref, stats_ref, full_ref, column_ref):
     units = mine_ref.shape[1]
-    own = solution_ref.shape[1]
+    own = solution_ref.shape[0]
     src = lax.axis_index("src")
     half = ROWS // 2
     bit = src % 2
@@ -138,8 +138,17 @@
     weight = jnp.sum(full_ref[ROW_WEIGHT:ROW_WEIGHT + 1, :], axis=1, keepdims=True)
     stats_ref[...] = jnp.where(lax.broadcasted_iota(jnp.int32, (8, 128), 0) == 0, chi, weight)
     shift = (units - src * own) % units
-    solution_ref[0:8, :] = pltpu.roll(low_x, shift, 1)[:, :own]
-    solution_ref[8:16, :] = pltpu.roll(high_x, shift, 1)[:, :own]
+    turned = pltpu.roll(jnp.concatenate([low_x, high_x], axis=0), shift, 1)
+    solution_ref[...] = turned[:, :128].T[:own]
+
+
+def quotient_kernel(own_ref, other_ref, out_ref):
+    total = own_ref[...] + other_ref[...]
+    out_ref[...] = total[0:1, 0:1] / total[1:2, 0:1]
+
+
+def in_vmem(x):
+    return pltpu.with_memory_space_constraint(x, pltpu.VMEM)
 
 
 def swap(x, axis, mask):
@@ -151,7 +160,7 @@
     masks = []
     b = 1
     while (1 << b) < size:
-        masks.append((1 << b) if b < 3 else (1 << b) | (1 << (b - 1)))
+        masks.append(1 << b)
         b += 1
     return masks
 
@@ -168,33 +177,42 @@
         accumulate_kernel,
         grid=(slots // chunk,),
         in_specs=[
-            pl.BlockSpec(memory_space=pltpu.SMEM),
+            pl.BlockSpec((1, 1), lambda s: (0, 0)),
             pl.BlockSpec((16, chunk), lambda s: (0, s)),
             line(), line(), line(),
             pl.BlockSpec((1, own_units), lambda s: (0, 0)),
         ],
-        out_specs=[pl.BlockSpec((half, units), lambda s: (0, 0))] * 2,
-        out_shape=[jax.ShapeDtypeStruct((half, units), jnp.float32)] * 2,
+        out_specs=[pl.BlockSpec(memory_space=pltpu.VMEM)] * 2,
+        out_shape=[pltpu.VMEM((half, units), jnp.float32)] * 2,
         scratch_shapes=[pltpu.VMEM((ROWS, units), jnp.float32), pltpu.VMEM((8, 128), jnp.float32)],
         compiler_params=pltpu.CompilerParams(dimension_semantics=("arbitrary",)),
         name="accumulate",
-    )(obs_count, design, unit_index.reshape(1, slots), residual.reshape(1, slots), weight.reshape(1, slots), damping.reshape(1, own_units))
+    )(obs_count.reshape(1, 1), design, unit_index.reshape(1, slots), residual.reshape(1, slots), weight.reshape(1, slots), damping.reshape(1, own_units))
     mine = keep + swap(send, "src", 1)
     for mask in masks_of(n_source):
         mine = mine + swap(mine, "src", mask)
     other = swap(mine, "src", 1)
     solution_own, stats = pl.pallas_call(
         solve_kernel,
-        out_shape=[jax.ShapeDtypeStruct((16, own_units), jnp.float32), jax.ShapeDtypeStruct((8, 128), jnp.float32)],
+        in_specs=[pl.BlockSpec(memory_space=pltpu.VMEM)] * 2,
+        out_specs=[pl.BlockSpec(memory_space=pltpu.VMEM)] * 2,
+        out_shape=[jax.ShapeDtypeStruct((own_units, 16), jnp.float32), pltpu.VMEM((8, 128), jnp.float32)],
         scratch_shapes=[pltpu.VMEM((ROWS, units), jnp.float32), pltpu.VMEM((16 * 24, units), jnp.float32)],
         name="solve",
-    )(mine, other)
+    )(in_vmem(mine), in_vmem(other))
     n_time = lax.axis_size("tm")
     mask = 1
-    while mask < n_time:
+    while 2 * mask < n_time:
         stats = stats + swap(stats, "tm", mask)
         mask *= 2
-    return (solution_own, stats[0, 0] / stats[1, 0])
+    last = swap(stats, "tm", mask) if n_time > 1 else jnp.zeros_like(stats)
+    misfit = pl.pallas_call(
+        quotient_kernel,
+        in_specs=[pl.BlockSpec(memory_space=pltpu.VMEM)] * 2,
+        out_shape=jax.ShapeDtypeStruct((1, 1), jnp.float32),
+        name="quotient",
+    )(in_vmem(stats), in_vmem(last))
+    return (solution_own.T, misfit.reshape(()))
 
 
 def solution(mesh):

time: 35.1 us -> 28.2 us (0.80)
  local copies, waits for them, and re-layouts: 2.56 us -> 0 us
  between operations: 3.74 us -> 1.29 us
  starting transfers between devices: 11.3 us -> 10.3 us
  waiting for transfers between devices: 8.98 us -> 9.8 us
  Pallas kernels: 7.38 us -> 6.57 us
  other arithmetic: 0.81 us -> 0.03 us
    unnamed x7 -> x0, local copies, waits for them, and re-layouts: 1.98 us -> none
    ppermute x6, starting transfers between devices: 11.3 us -> 10.3 us  [swap(): return lax.ppermute(x, axis, [(k, k ^ mask) for k in range(size)])]
    ppermute x6, waiting for transfers between devices: 8.98 us -> 9.8 us  [swap(): return lax.ppermute(x, axis, [(k, k ^ mask) for k in range(size)])]
    add x1, other arithmetic: 0.78 us -> 0.01 us  [on_device(): mine = keep + swap(send, 'src', 1)]
    slice x1 -> x0, local copies, waits for them, and re-layouts: 0.58 us -> none  [on_device(): return (solution_own, stats[0, 0] / stats[1, 0])]
    pallas_call x1, Pallas kernels: 5.43 us -> 4.87 us  [on_device(): pl.pallas_call(accumulate_kernel, grid=(slots // chunk,), in_specs=[pl.Bl...]
    pallas_call x1 -> x2, Pallas kernels: 1.95 us -> 1.71 us  [the longest x1 1.19 us: on_device(): pl.pallas_call(solve_kernel, in_specs=[pl.BlockSpec(memory_space=pltpu.VM...]
  transfers between devices with their start and end apart: 6 -> 6, of which waited for: 6 -> 6; matrix products, arithmetic and copies ran while one was open for 4% -> 0% of each run, Pallas kernels for 0% -> 0%
where the time goes in v2:
time: 28.2 us; the launch traced here: 28 us
  starting transfers between devices  10.3 us (37%)
  waiting for transfers between devices  9.8 us (35%)
  Pallas kernels  6.57 us (23%)
  between operations  1.29 us (5%)
    ppermute x6, starting transfers between devices, swap(): return lax.ppermute(x, axis, [(k, k ^ mask) for k in range(size)])  10.3 us
    ppermute x6, waiting for transfers between devices, swap(): return lax.ppermute(x, axis, [(k, k ^ mask) for k in range(size)])  9.8 us
    pallas_call x1, Pallas kernels, on_device(): pl.pallas_call(accumulate_kernel, grid=(slots // chunk,), in_specs=[pl.Bl...  4.87 us
    pallas_call x1, Pallas kernels, on_device(): pl.pallas_call(solve_kernel, in_specs=[pl.BlockSpec(memory_space=pltpu.VM...  1.19 us
  transfers between devices with their start and end apart: 6, of which 6 were waited for; matrix products, arithmetic and copies ran while one was open for 0% of the time, Pallas kernels for 0%

profile of v2, /device:TPU:0, one launch (start us, length us, event | category | flops | bytes accessed | tf_op | source)
XLA Modules:
  0.0 28.0 jit_solution(5162221266076453946)
XLA Ops:
  1.3 4.9 %accumulate.1 = (f32[80,128]{1,0:T(8,128)S(1)}, f32[80,128]{1,0:T(8,128)S(1)}) custom-call(s32[1,1]{1,0:T(1,128)} %bitcast.7.count_ref, f32[16,16384]{1,0:T(8,128)} %design_ref.1, s32[1,16384]{1,0:T(1,128)} %bitcast.8, f32[1,16384]{1,0:T(1,128)} %bitcast.9, f32[1,16384]{1,0:T(1,128)} %bitcast.10, f32[1,8]{1,0:T(1,128)} %bitcast.11), custom_call_target="tpu_custom_call" | custom-call | tf_op jit(solution)/shard_map/accumulate/pallas_call | solution.py:176
  6.1 0.5 %collective-permute-start = (f32[80,128]{1,0:T(8,128)S(1)}, f32[80,128]{1,0:T(8,128)S(1)}, u32[]{:S(2)}, u32[]{:S(2)}) collective-permute-start(f32[80,128]{1,0:T(8,128)S(1)} %get-tuple-element.7), channel_id=1, source_target_pairs={{0,1},{1,0},{2,3},{3,2},{4,5},{5,4},{6,7},{7,6},{8,9},{9,8},{10,11... | collective-permute-start | bytes 122888 | tf_op jit(solution)/shard_map/ppermute | solution.py:156
  6.7 0.9 %collective-permute-done = f32[80,128]{1,0:T(8,128)S(1)} collective-permute-done((f32[80,128]{1,0:T(8,128)S(1)}, f32[80,128]{1,0:T(8,128)S(1)}, u32[]{:S(2)}, u32[]{:S(2)}) %collective-permute-start) | collective-permute-done | bytes 40992 | tf_op jit(solution)/shard_map/ppermute | solution.py:156
  7.6 2.8 %collective-permute-start.1 = (f32[80,128]{1,0:T(8,128)S(1)}, f32[80,128]{1,0:T(8,128)S(1)}, u32[]{:S(2)}, u32[]{:S(2)}) collective-permute-start(f32[80,128]{1,0:T(8,128)S(1)} %add.12), channel_id=1, source_target_pairs={{0,2},{1,3},{2,0},{3,1},{4,6},{5,7},{6,4},{7,5},{8,10},{9,11},{10,... | collective-permute-start | bytes 122888 | tf_op jit(solution)/shard_map/ppermute | solution.py:156
  10.4 2.0 %collective-permute-done.1 = f32[80,128]{1,0:T(8,128)S(1)} collective-permute-done((f32[80,128]{1,0:T(8,128)S(1)}, f32[80,128]{1,0:T(8,128)S(1)}, u32[]{:S(2)}, u32[]{:S(2)}) %collective-permute-start.1) | collective-permute-done | bytes 40992 | tf_op jit(solution)/shard_map/ppermute | solution.py:156
  12.4 2.1 %collective-permute-start.2 = (f32[80,128]{1,0:T(8,128)S(1)}, f32[80,128]{1,0:T(8,128)S(1)}, u32[]{:S(2)}, u32[]{:S(2)}) collective-permute-start(f32[80,128]{1,0:T(8,128)S(1)} %add.13), channel_id=1, source_target_pairs={{0,4},{1,5},{2,6},{3,7},{4,0},{5,1},{6,2},{7,3},{8,12},{9,13},{10,... | collective-permute-start | bytes 122888 | tf_op jit(solution)/shard_map/ppermute | solution.py:156
  14.5 2.0 %collective-permute-done.2 = f32[80,128]{1,0:T(8,128)S(1)} collective-permute-done((f32[80,128]{1,0:T(8,128)S(1)}, f32[80,128]{1,0:T(8,128)S(1)}, u32[]{:S(2)}, u32[]{:S(2)}) %collective-permute-start.2) | collective-permute-done | bytes 40992 | tf_op jit(solution)/shard_map/ppermute | solution.py:156
  16.5 3.0 %collective-permute-start.3 = (f32[80,128]{1,0:T(8,128)S(1)}, f32[80,128]{1,0:T(8,128)S(1)}, u32[]{:S(2)}, u32[]{:S(2)}) collective-permute-start(f32[80,128]{1,0:T(8,128)S(1)} %add.14), channel_id=1, source_target_pairs={{0,8},{1,9},{2,10},{3,11},{4,12},{5,13},{6,14},{7,15},{8,0},{9,1},... | collective-permute-start | bytes 122888 | tf_op jit(solution)/shard_map/ppermute | solution.py:156
  19.5 2.0 %collective-permute-done.3 = f32[80,128]{1,0:T(8,128)S(1)} collective-permute-done((f32[80,128]{1,0:T(8,128)S(1)}, f32[80,128]{1,0:T(8,128)S(1)}, u32[]{:S(2)}, u32[]{:S(2)}) %collective-permute-start.3) | collective-permute-done | bytes 40992 | tf_op jit(solution)/shard_map/ppermute | solution.py:156
  21.5 0.0 collective-permute-start.4
  21.5 1.2 %collective-permute-done.4.other_ref = f32[80,128]{1,0:T(8,128)S(1)} collective-permute-done((f32[80,128]{1,0:T(8,128)S(1)}, f32[80,128]{1,0:T(8,128)S(1)}, u32[]{:S(2)}, u32[]{:S(2)}) %collective-permute-start.4) | collective-permute-done | bytes 40992 | tf_op jit(solution)/shard_map/ppermute | solution.py:156
  22.7 1.2 %solve.1 = (f32[8,16]{1,0:T(8,128)}, f32[8,128]{1,0:T(8,128)S(1)}) custom-call(f32[80,128]{1,0:T(8,128)S(1)} %add.15.mine_ref, f32[80,128]{1,0:T(8,128)S(1)} %collective-permute-done.4.other_ref), custom_call_target="tpu_custom_call" | custom-call | tf_op jit(solution)/shard_map/solve/pallas_call | solution.py:195
  23.9 1.8 %collective-permute-start.5 = (f32[8,128]{1,0:T(8,128)S(1)}, f32[8,128]{1,0:T(8,128)S(1)}, u32[]{:S(2)}, u32[]{:S(2)}) collective-permute-start(f32[8,128]{1,0:T(8,128)S(1)} %get-tuple-element.9.own_ref), channel_id=1, source_target_pairs={{0,16},{16,0},{1,17},{17,1},{2,18},{18,2},{3,19},{19,3},{4,20},{20... | collective-permute-start | bytes 12296 | tf_op jit(solution)/shard_map/ppermute | solution.py:156
  25.7 1.8 %collective-permute-done.5.other_ref = f32[8,128]{1,0:T(8,128)S(1)} collective-permute-done((f32[8,128]{1,0:T(8,128)S(1)}, f32[8,128]{1,0:T(8,128)S(1)}, u32[]{:S(2)}, u32[]{:S(2)}) %collective-permute-start.5) | collective-permute-done | bytes 4128 | tf_op jit(solution)/shard_map/ppermute | solution.py:156
  27.5 0.5 %quotient.1 = f32[1,1]{1,0:T(1,128)} custom-call(f32[8,128]{1,0:T(8,128)S(1)} %get-tuple-element.9.own_ref, f32[8,128]{1,0:T(8,128)S(1)} %collective-permute-done.5.other_ref), custom_call_target="tpu_custom_call" | custom-call | tf_op jit(solution)/shard_map/quotient/pallas_call | solution.py:209
  (4 shorter events, 0.0 us)
Async XLA Ops:
  6.1 1.4 %collective-permute-start = (f32[80,128]{1,0:T(8,128)S(1)}, f32[80,128]{1,0:T(8,128)S(1)}, u32[]{:S(2)}, u32[]{:S(2)}) collective-permute-start(f32[80,128]{1,0:T(8,128)S(1)} %get-tuple-element.7), channel_id=1, source_target_pairs={{0,1},{1,0},{2,3},{3,2},{4,5},{5,4},{6,7},{7,6},{8,9},{9,8},{10,11... | collective-permute-start | bytes 122888 | tf_op jit(solution)/shard_map/ppermute | solution.py:156
  7.6 4.8 %collective-permute-start.1 = (f32[80,128]{1,0:T(8,128)S(1)}, f32[80,128]{1,0:T(8,128)S(1)}, u32[]{:S(2)}, u32[]{:S(2)}) collective-permute-start(f32[80,128]{1,0:T(8,128)S(1)} %add.12), channel_id=1, source_target_pairs={{0,2},{1,3},{2,0},{3,1},{4,6},{5,7},{6,4},{7,5},{8,10},{9,11},{10,... | collective-permute-start | bytes 122888 | tf_op jit(solution)/shard_map/ppermute | solution.py:156
  12.4 4.1 %collective-permute-start.2 = (f32[80,128]{1,0:T(8,128)S(1)}, f32[80,128]{1,0:T(8,128)S(1)}, u32[]{:S(2)}, u32[]{:S(2)}) collective-permute-start(f32[80,128]{1,0:T(8,128)S(1)} %add.13), channel_id=1, source_target_pairs={{0,4},{1,5},{2,6},{3,7},{4,0},{5,1},{6,2},{7,3},{8,12},{9,13},{10,... | collective-permute-start | bytes 122888 | tf_op jit(solution)/shard_map/ppermute | solution.py:156
  16.5 5.0 %collective-permute-start.3 = (f32[80,128]{1,0:T(8,128)S(1)}, f32[80,128]{1,0:T(8,128)S(1)}, u32[]{:S(2)}, u32[]{:S(2)}) collective-permute-start(f32[80,128]{1,0:T(8,128)S(1)} %add.14), channel_id=1, source_target_pairs={{0,8},{1,9},{2,10},{3,11},{4,12},{5,13},{6,14},{7,15},{8,0},{9,1},... | collective-permute-start | bytes 122888 | tf_op jit(solution)/shard_map/ppermute | solution.py:156
  21.5 1.2 %collective-permute-start.4 = (f32[80,128]{1,0:T(8,128)S(1)}, f32[80,128]{1,0:T(8,128)S(1)}, u32[]{:S(2)}, u32[]{:S(2)}) collective-permute-start(f32[80,128]{1,0:T(8,128)S(1)} %add.15.mine_ref), channel_id=1, source_target_pairs={{0,1},{1,0},{2,3},{3,2},{4,5},{5,4},{6,7},{7,6},{8,9},{9,8},{10,11... | collective-permute-start | bytes 122888 | tf_op jit(solution)/shard_map/ppermute | solution.py:156
  23.9 3.6 %collective-permute-start.5 = (f32[8,128]{1,0:T(8,128)S(1)}, f32[8,128]{1,0:T(8,128)S(1)}, u32[]{:S(2)}, u32[]{:S(2)}) collective-permute-start(f32[8,128]{1,0:T(8,128)S(1)} %get-tuple-element.9.own_ref), channel_id=1, source_target_pairs={{0,16},{16,0},{1,17},{17,1},{2,18},{18,2},{3,19},{19,3},{4,20},{20... | collective-permute-start | bytes 12296 | tf_op jit(solution)/shard_map/ppermute | solution.py:156

commit v3 on v2

--- a/solution.py
+++ b/solution.py
@@ -9,7 +9,7 @@
 CROSS = 8
 ROWS = 160
 ROW_WEIGHT, ROW_BEFORE, ROW_DAMPING = 36, 37, 38
-CHUNK = 8192
+EDGES = (0, 8)
 PIECE = 2048
 
 
@@ -22,26 +22,43 @@
     return 80 + ((i - 8 - j) % 8) * 8 + j
 
 
-def accumulate_kernel(count_ref, design_ref, unit_ref, resid_ref, weight_ref, damping_ref, keep_ref, send_ref, acc_ref, side_ref):
-    step = pl.program_id(0)
-    chunk = design_ref.shape[1]
+def accumulate_kernel(count_hbm, design_hbm, unit_hbm, resid_hbm, weight_hbm, damping_hbm, keep_ref, send_ref, count_ref, design_ref, unit_ref, resid_ref, weight_ref, damping_ref, acc_ref, sems, small_sems):
+    slots = design_ref.shape[1]
     units = acc_ref.shape[1]
-    piece = min(PIECE, chunk)
     src = lax.axis_index("src")
     first_unit = lax.axis_index("tm") * units
-    count = count_ref[...]
-
-    @pl.when(step == 0)
-    def _():
-        acc_ref[...] = jnp.zeros_like(acc_ref)
-        side_ref[...] = jnp.zeros_like(side_ref)
-
-    unit_rows = lax.broadcasted_iota(jnp.int32, (units, piece), 0)
-    slot = lax.broadcasted_iota(jnp.int32, (1, piece), 1) + step * chunk
+    edges = [slots * e // 8 for e in EDGES]
+    copies = [
+        [
+            pltpu.make_async_copy(hbm.at[:, pl.ds(lo, hi - lo)], ref.at[:, pl.ds(lo, hi - lo)], sems.at[c, n])
+            for n, (hbm, ref) in enumerate(
+                [(weight_hbm, weight_ref), (unit_hbm, unit_ref), (resid_hbm, resid_ref), (design_hbm, design_ref)]
+            )
+        ]
+        for c, (lo, hi) in enumerate(zip(edges[:-1], edges[1:]))
+    ]
+    count_copy = pltpu.make_async_copy(count_hbm, count_ref, small_sems.at[0])
+    damping_copy = pltpu.make_async_copy(damping_hbm, damping_ref, small_sems.at[1])
+    count_copy.start()
+    for group in copies:
+        for copy in group:
+            copy.start()
+    damping_copy.start()
+    count_copy.wait()
+    count = count_ref[0]
+    piece = min(PIECE, edges[1])
+    own = damping_ref.shape[1]
+    middle = units // 2
+    inner = lax.broadcasted_iota(jnp.int32, (own, piece), 0)
+    unit_rows = jnp.concatenate([inner + k * own for k in [*range(0, units // own, 2), *range(1, units // own, 2)]], axis=0)
+    slot = lax.broadcasted_iota(jnp.int32, (1, piece), 1)
     total = jnp.zeros((2 * ROWS, units), jnp.float32)
     weight_sum = jnp.zeros((1, 128), jnp.float32)
     before_sum = jnp.zeros((1, 128), jnp.float32)
-    for begin in range(0, chunk, piece):
+    for begin in range(0, slots, piece):
+        if begin in edges:
+            for copy in copies[edges.index(begin)]:
+                copy.wait()
         at = pl.ds(begin, piece)
         rows = design_ref[:, at]
         resid = resid_ref[:, at]
@@ -67,32 +84,33 @@
         for k in range(0, piece, 128):
             weight_sum = weight_sum + weight[:, k:k + 128]
             before_sum = before_sum + before[:, k:k + 128]
-    acc_ref[...] += total[:ROWS] + total[ROWS:]
-    side_ref[0:1] += weight_sum
-    side_ref[1:2] += before_sum
-
-    @pl.when(step == pl.num_programs(0) - 1)
-    def _():
-        acc_ref[ROW_WEIGHT:ROW_DAMPING + 1, :] = jnp.zeros((3, units), jnp.float32)
-        acc_ref[ROW_WEIGHT:ROW_BEFORE + 1, 0:128] = side_ref[0:2]
-        own = damping_ref.shape[1]
-        padded = jnp.concatenate([damping_ref[...], jnp.zeros((1, units - own), jnp.float32)], axis=1)
-        placed = pltpu.roll(jnp.broadcast_to(padded, (8, units)), src * own, 1)
-        acc_ref[ROW_DAMPING:ROW_DAMPING + 1, :] = placed[0:1]
-        half = ROWS // 2
-        bit = src % 2
-        keep_ref[...] = acc_ref[pl.ds(pl.multiple_of(bit * half, 8), half), :]
-        send_ref[...] = acc_ref[pl.ds(pl.multiple_of((1 - bit) * half, 8), half), :]
-
-
-def solve_kernel(mine_ref, other_ref, solution_ref, stats_ref, full_ref, column_ref):
+    acc_ref[...] = total[:ROWS] + total[ROWS:]
+    acc_ref[ROW_WEIGHT:ROW_DAMPING + 1, :] = jnp.zeros((3, units), jnp.float32)
+    acc_ref[ROW_WEIGHT:ROW_WEIGHT + 1, 0:128] = weight_sum
+    acc_ref[ROW_BEFORE:ROW_BEFORE + 1, 0:128] = before_sum
+    damping_copy.wait()
+    padded = jnp.concatenate([damping_ref[...], jnp.zeros((1, units - own), jnp.float32)], axis=1)
+    placed = pltpu.roll(jnp.broadcast_to(padded, (8, units)), (src // 2) * own + (src % 2) * middle, 1)
+    acc_ref[ROW_DAMPING:ROW_DAMPING + 1, :] = placed[0:1]
+    half = ROWS // 2
+    plain = acc_ref[...]
+    turned = pltpu.roll(plain, middle, 1)
+    lanes = lax.broadcasted_iota(jnp.int32, (half, units), 1) < middle
+    even = jnp.where(lanes, plain[:half], turned[half:])
+    odd = jnp.where(lanes, turned[:half], plain[half:])
+    is_even = src % 2 == 0
+    keep_ref[...] = jnp.where(is_even, even, odd)
+    send_ref[...] = jnp.where(is_even, odd, even)
+
+
+def solve_kernel(mine_ref, solution_ref, stats_ref, full_ref, column_ref):
     units = mine_ref.shape[1]
     own = solution_ref.shape[0]
     src = lax.axis_index("src")
     half = ROWS // 2
-    bit = src % 2
-    full_ref[pl.ds(pl.multiple_of(bit * half, 8), half), :] = mine_ref[...]
-    full_ref[pl.ds(pl.multiple_of((1 - bit) * half, 8), half), :] = other_ref[...]
+    middle = units // 2
+    full_ref[:half, :] = mine_ref[...]
+    full_ref[half:, :] = pltpu.roll(mine_ref[...], middle, 1)
     column_ref[...] = jnp.zeros_like(column_ref)
     for j in range(16):
         for i in range(j, 16):
@@ -134,17 +152,20 @@
     squares = damping * jnp.sum(low_x * low_x + high_x * high_x, axis=0, keepdims=True)
     for y in forward:
         squares = squares + y * y
-    chi = jnp.sum(full_ref[ROW_BEFORE:ROW_BEFORE + 1, :] - squares, axis=1, keepdims=True)
-    weight = jnp.sum(full_ref[ROW_WEIGHT:ROW_WEIGHT + 1, :], axis=1, keepdims=True)
+    held = lax.broadcasted_iota(jnp.int32, (1, units), 1) < middle
+    chi = jnp.sum(jnp.where(held, full_ref[ROW_BEFORE:ROW_BEFORE + 1, :] - squares, 0.0), axis=1, keepdims=True)
+    weight = jnp.sum(jnp.where(held, full_ref[ROW_WEIGHT:ROW_WEIGHT + 1, :], 0.0), axis=1, keepdims=True)
     stats_ref[...] = jnp.where(lax.broadcasted_iota(jnp.int32, (8, 128), 0) == 0, chi, weight)
-    shift = (units - src * own) % units
+    shift = (units - (src // 2) * own) % units
     turned = pltpu.roll(jnp.concatenate([low_x, high_x], axis=0), shift, 1)
     solution_ref[...] = turned[:, :128].T[:own]
 
 
-def quotient_kernel(own_ref, other_ref, out_ref):
-    total = own_ref[...] + other_ref[...]
-    out_ref[...] = total[0:1, 0:1] / total[1:2, 0:1]
+def quotient_kernel(*refs):
+    parts = [ref[...] for ref in refs[:-1]]
+    while len(parts) > 1:
+        parts = [a + b for a, b in zip(parts[::2], parts[1::2])]
+    refs[-1][...] = parts[0][0:1, 0:1] / parts[0][1:2, 0:1]
 
 
 def in_vmem(x):
@@ -170,48 +191,53 @@
     own_units = damping.shape[0]
     units = own_units * n_source
     slots = design.shape[1]
-    chunk = min(CHUNK, slots)
     half = ROWS // 2
-    line = lambda: pl.BlockSpec((1, chunk), lambda s: (0, s))
     keep, send = pl.pallas_call(
         accumulate_kernel,
-        grid=(slots // chunk,),
-        in_specs=[
-            pl.BlockSpec((1, 1), lambda s: (0, 0)),
-            pl.BlockSpec((16, chunk), lambda s: (0, s)),
-            line(), line(), line(),
-            pl.BlockSpec((1, own_units), lambda s: (0, 0)),
-        ],
+        in_specs=[pl.BlockSpec(memory_space=pltpu.HBM)] * 6,
         out_specs=[pl.BlockSpec(memory_space=pltpu.VMEM)] * 2,
         out_shape=[pltpu.VMEM((half, units), jnp.float32)] * 2,
-        scratch_shapes=[pltpu.VMEM((ROWS, units), jnp.float32), pltpu.VMEM((8, 128), jnp.float32)],
-        compiler_params=pltpu.CompilerParams(dimension_semantics=("arbitrary",)),
+        scratch_shapes=[
+            pltpu.SMEM((1,), jnp.int32),
+            pltpu.VMEM((16, slots), jnp.float32),
+            pltpu.VMEM((1, slots), jnp.int32),
+            pltpu.VMEM((1, slots), jnp.float32),
+            pltpu.VMEM((1, slots), jnp.float32),
+            pltpu.VMEM((1, own_units), jnp.float32),
+            pltpu.VMEM((ROWS, units), jnp.float32),
+            pltpu.SemaphoreType.DMA((len(EDGES) - 1, 4)),
+            pltpu.SemaphoreType.DMA((2,)),
+        ],
         name="accumulate",
-    )(obs_count.reshape(1, 1), design, unit_index.reshape(1, slots), residual.reshape(1, slots), weight.reshape(1, slots), damping.reshape(1, own_units))
+    )(obs_count, design, unit_index.reshape(1, slots), residual.reshape(1, slots), weight.reshape(1, slots), damping.reshape(1, own_units))
     mine = keep + swap(send, "src", 1)
     for mask in masks_of(n_source):
         mine = mine + swap(mine, "src", mask)
-    other = swap(mine, "src", 1)
     solution_own, stats = pl.pallas_call(
         solve_kernel,
-        in_specs=[pl.BlockSpec(memory_space=pltpu.VMEM)] * 2,
+        in_specs=[pl.BlockSpec(memory_space=pltpu.VMEM)],
         out_specs=[pl.BlockSpec(memory_space=pltpu.VMEM)] * 2,
         out_shape=[jax.ShapeDtypeStruct((own_units, 16), jnp.float32), pltpu.VMEM((8, 128), jnp.float32)],
         scratch_shapes=[pltpu.VMEM((ROWS, units), jnp.float32), pltpu.VMEM((16 * 24, units), jnp.float32)],
         name="solve",
-    )(in_vmem(mine), in_vmem(other))
+    )(in_vmem(mine))
     n_time = lax.axis_size("tm")
-    mask = 1
-    while 2 * mask < n_time:
-        stats = stats + swap(stats, "tm", mask)
-        mask *= 2
-    last = swap(stats, "tm", mask) if n_time > 1 else jnp.zeros_like(stats)
+    if n_time == 2:
+        across = [(t * n_source + k, (t ^ 1) * n_source + (k ^ 1)) for t in range(2) for k in range(n_source)]
+        parts = [stats, swap(stats, "src", 1), swap(stats, "tm", 1), lax.ppermute(stats, ("tm", "src"), across)]
+    else:
+        stats = stats + swap(stats, "src", 1)
+        mask = 1
+        while 2 * mask < n_time:
+            stats = stats + swap(stats, "tm", mask)
+            mask *= 2
+        parts = [stats, swap(stats, "tm", mask)] if n_time > 1 else [stats]
     misfit = pl.pallas_call(
         quotient_kernel,
-        in_specs=[pl.BlockSpec(memory_space=pltpu.VMEM)] * 2,
+        in_specs=[pl.BlockSpec(memory_space=pltpu.VMEM)] * len(parts),
         out_shape=jax.ShapeDtypeStruct((1, 1), jnp.float32),
         name="quotient",
-    )(in_vmem(stats), in_vmem(last))
+    )(*[in_vmem(part) for part in parts])
     return (solution_own.T, misfit.reshape(()))
 
 

time: 28.2 us -> 26.8 us (0.950)
  waiting for transfers between devices: 9.8 us -> 8.48 us
  Pallas kernels: 6.57 us -> 6.13 us
    ppermute x6, waiting for transfers between devices: 9.8 us -> 7.39 us  [swap(): return lax.ppermute(x, axis, [(k, k ^ mask) for k in range(size)])]
    ppermute x0 -> x1, waiting for transfers between devices: none -> 1.09 us  [on_device(): lax.ppermute(stats, ('tm', 'src'), across)]
    pallas_call x1, Pallas kernels: 4.87 us -> 4.43 us  [on_device(): pl.pallas_call(accumulate_kernel, in_specs=[pl.BlockSpec(memory_space=plt...]
  transfers between devices with their start and end apart: 6 -> 7, of which waited for: 6 -> 6; matrix products, arithmetic and copies ran while one was open for 0% -> 0% of each run, Pallas kernels for 0% -> 0%
where the time goes in v3:
time: 26.8 us; the launch traced here: 26.4 us
  starting transfers between devices  10.5 us (39%)
  waiting for transfers between devices  8.48 us (32%)
  Pallas kernels  6.13 us (23%)
  between operations  1.3 us (5%)
    ppermute x6, starting transfers between devices, swap(): return lax.ppermute(x, axis, [(k, k ^ mask) for k in range(size)])  10.5 us
    ppermute x6, waiting for transfers between devices, swap(): return lax.ppermute(x, axis, [(k, k ^ mask) for k in range(size)])  7.39 us
    pallas_call x1, Pallas kernels, on_device(): pl.pallas_call(accumulate_kernel, in_specs=[pl.BlockSpec(memory_space=plt...  4.43 us
    pallas_call x1, Pallas kernels, on_device(): pl.pallas_call(solve_kernel, in_specs=[pl.BlockSpec(memory_space=pltpu.VM...  1.17 us
    ppermute x1, waiting for transfers between devices, on_device(): lax.ppermute(stats, ('tm', 'src'), across)  1.09 us
  transfers between devices with their start and end apart: 7, of which 6 were waited for; matrix products, arithmetic and copies ran while one was open for 0% of the time, Pallas kernels for 0%

profile of v3, /device:TPU:0, one launch (start us, length us, event | category | flops | bytes accessed | tf_op | source)
XLA Modules:
  0.0 26.4 jit_solution(6908148999294032545)
XLA Ops:
  1.3 4.4 %accumulate.1 = (f32[80,128]{1,0:T(8,128)S(1)}, f32[80,128]{1,0:T(8,128)S(1)}) custom-call(s32[1]{0:T(128)S(6)} %copy.8.count_hbm, f32[16,16384]{1,0:T(8,128)} %design_hbm.1, s32[1,16384]{1,0:T(1,128)} %bitcast.6, f32[1,16384]{1,0:T(1,128)} %bitcast.7, f32[1,16384]{1,0:T(1,128)} %bitcast.8, f32[1,8]{1,0:T(1,128)} %bitcast.9), custom_call_target="tpu_custom_call" | custom-call | tf_op jit(solution)/shard_map/accumulate/pallas_call | solution.py:195
  5.7 0.6 %collective-permute-start = (f32[80,128]{1,0:T(8,128)S(1)}, f32[80,128]{1,0:T(8,128)S(1)}, u32[]{:S(2)}, u32[]{:S(2)}) collective-permute-start(f32[80,128]{1,0:T(8,128)S(1)} %get-tuple-element.7), channel_id=1, source_target_pairs={{0,1},{1,0},{2,3},{3,2},{4,5},{5,4},{6,7},{7,6},{8,9},{9,8},{10,11... | collective-permute-start | bytes 122888 | tf_op jit(solution)/shard_map/ppermute | solution.py:177
  6.3 0.9 %collective-permute-done = f32[80,128]{1,0:T(8,128)S(1)} collective-permute-done((f32[80,128]{1,0:T(8,128)S(1)}, f32[80,128]{1,0:T(8,128)S(1)}, u32[]{:S(2)}, u32[]{:S(2)}) %collective-permute-start) | collective-permute-done | bytes 40992 | tf_op jit(solution)/shard_map/ppermute | solution.py:177
  7.1 2.9 %collective-permute-start.1 = (f32[80,128]{1,0:T(8,128)S(1)}, f32[80,128]{1,0:T(8,128)S(1)}, u32[]{:S(2)}, u32[]{:S(2)}) collective-permute-start(f32[80,128]{1,0:T(8,128)S(1)} %add.12), channel_id=1, source_target_pairs={{0,2},{1,3},{2,0},{3,1},{4,6},{5,7},{6,4},{7,5},{8,10},{9,11},{10,... | collective-permute-start | bytes 122888 | tf_op jit(solution)/shard_map/ppermute | solution.py:177
  10.0 2.0 %collective-permute-done.1 = f32[80,128]{1,0:T(8,128)S(1)} collective-permute-done((f32[80,128]{1,0:T(8,128)S(1)}, f32[80,128]{1,0:T(8,128)S(1)}, u32[]{:S(2)}, u32[]{:S(2)}) %collective-permute-start.1) | collective-permute-done | bytes 40992 | tf_op jit(solution)/shard_map/ppermute | solution.py:177
  12.0 2.1 %collective-permute-start.2 = (f32[80,128]{1,0:T(8,128)S(1)}, f32[80,128]{1,0:T(8,128)S(1)}, u32[]{:S(2)}, u32[]{:S(2)}) collective-permute-start(f32[80,128]{1,0:T(8,128)S(1)} %add.13), channel_id=1, source_target_pairs={{0,4},{1,5},{2,6},{3,7},{4,0},{5,1},{6,2},{7,3},{8,12},{9,13},{10,... | collective-permute-start | bytes 122888 | tf_op jit(solution)/shard_map/ppermute | solution.py:177
  14.1 2.0 %collective-permute-done.2 = f32[80,128]{1,0:T(8,128)S(1)} collective-permute-done((f32[80,128]{1,0:T(8,128)S(1)}, f32[80,128]{1,0:T(8,128)S(1)}, u32[]{:S(2)}, u32[]{:S(2)}) %collective-permute-start.2) | collective-permute-done | bytes 40992 | tf_op jit(solution)/shard_map/ppermute | solution.py:177
  16.1 3.0 %collective-permute-start.3 = (f32[80,128]{1,0:T(8,128)S(1)}, f32[80,128]{1,0:T(8,128)S(1)}, u32[]{:S(2)}, u32[]{:S(2)}) collective-permute-start(f32[80,128]{1,0:T(8,128)S(1)} %add.14), channel_id=1, source_target_pairs={{0,8},{1,9},{2,10},{3,11},{4,12},{5,13},{6,14},{7,15},{8,0},{9,1},... | collective-permute-start | bytes 122888 | tf_op jit(solution)/shard_map/ppermute | solution.py:177
  19.1 2.0 %collective-permute-done.3 = f32[80,128]{1,0:T(8,128)S(1)} collective-permute-done((f32[80,128]{1,0:T(8,128)S(1)}, f32[80,128]{1,0:T(8,128)S(1)}, u32[]{:S(2)}, u32[]{:S(2)}) %collective-permute-start.3) | collective-permute-done | bytes 40992 | tf_op jit(solution)/shard_map/ppermute | solution.py:177
  21.1 1.2 %solve.1 = (f32[8,16]{1,0:T(8,128)}, f32[8,128]{1,0:T(8,128)S(1)}) custom-call(f32[80,128]{1,0:T(8,128)S(1)} %add.15.mine_ref), custom_call_target="tpu_custom_call" | custom-call | tf_op jit(solution)/shard_map/solve/pallas_call | solution.py:216
  22.3 0.0 collective-permute-start.6
  22.3 1.8 %collective-permute-start.5 = (f32[8,128]{1,0:T(8,128)S(1)}, f32[8,128]{1,0:T(8,128)S(1)}, u32[]{:S(2)}, u32[]{:S(2)}) collective-permute-start(f32[8,128]{1,0:T(8,128)S(1)} %get-tuple-element.9.refs_0_), channel_id=1, source_target_pairs={{0,16},{16,0},{1,17},{17,1},{2,18},{18,2},{3,19},{19,3},{4,20},{20... | collective-permute-start | bytes 12296 | tf_op jit(solution)/shard_map/ppermute | solution.py:177
  24.1 0.1 collective-permute-start.4
  24.2 1.1 %collective-permute-done.6.refs_3_ = f32[8,128]{1,0:T(8,128)S(1)} collective-permute-done((f32[8,128]{1,0:T(8,128)S(1)}, f32[8,128]{1,0:T(8,128)S(1)}, u32[]{:S(2)}, u32[]{:S(2)}) %collective-permute-start.6) | collective-permute-done | bytes 4128 | tf_op jit(solution)/shard_map/ppermute | solution.py:227
  25.3 0.6 %collective-permute-done.5.refs_2_ = f32[8,128]{1,0:T(8,128)S(1)} collective-permute-done((f32[8,128]{1,0:T(8,128)S(1)}, f32[8,128]{1,0:T(8,128)S(1)}, u32[]{:S(2)}, u32[]{:S(2)}) %collective-permute-start.5) | collective-permute-done | bytes 4128 | tf_op jit(solution)/shard_map/ppermute | solution.py:177
  25.9 0.0 collective-permute-done.4.refs_1_
  25.9 0.5 %quotient.1 = f32[1,1]{1,0:T(1,128)} custom-call(f32[8,128]{1,0:T(8,128)S(1)} %get-tuple-element.9.refs_0_, f32[8,128]{1,0:T(8,128)S(1)} %collective-permute-done.4.refs_1_, f32[8,128]{1,0:T(8,128)S(1)} %collective-permute-done.5.refs_2_, f32[8,128]{1,0:T(8,128)S(1)} %collective-permute-done.6.refs_3_), custom_call_target="tpu_custom_call" | custom-call | tf_op jit(solution)/shard_map/quotient/pallas_call | solution.py:235
  (4 shorter events, 0.0 us)
Async XLA Ops:
  5.7 1.4 %collective-permute-start = (f32[80,128]{1,0:T(8,128)S(1)}, f32[80,128]{1,0:T(8,128)S(1)}, u32[]{:S(2)}, u32[]{:S(2)}) collective-permute-start(f32[80,128]{1,0:T(8,128)S(1)} %get-tuple-element.7), channel_id=1, source_target_pairs={{0,1},{1,0},{2,3},{3,2},{4,5},{5,4},{6,7},{7,6},{8,9},{9,8},{10,11... | collective-permute-start | bytes 122888 | tf_op jit(solution)/shard_map/ppermute | solution.py:177
  7.1 4.8 %collective-permute-start.1 = (f32[80,128]{1,0:T(8,128)S(1)}, f32[80,128]{1,0:T(8,128)S(1)}, u32[]{:S(2)}, u32[]{:S(2)}) collective-permute-start(f32[80,128]{1,0:T(8,128)S(1)} %add.12), channel_id=1, source_target_pairs={{0,2},{1,3},{2,0},{3,1},{4,6},{5,7},{6,4},{7,5},{8,10},{9,11},{10,... | collective-permute-start | bytes 122888 | tf_op jit(solution)/shard_map/ppermute | solution.py:177
  12.0 4.1 %collective-permute-start.2 = (f32[80,128]{1,0:T(8,128)S(1)}, f32[80,128]{1,0:T(8,128)S(1)}, u32[]{:S(2)}, u32[]{:S(2)}) collective-permute-start(f32[80,128]{1,0:T(8,128)S(1)} %add.13), channel_id=1, source_target_pairs={{0,4},{1,5},{2,6},{3,7},{4,0},{5,1},{6,2},{7,3},{8,12},{9,13},{10,... | collective-permute-start | bytes 122888 | tf_op jit(solution)/shard_map/ppermute | solution.py:177
  16.1 5.0 %collective-permute-start.3 = (f32[80,128]{1,0:T(8,128)S(1)}, f32[80,128]{1,0:T(8,128)S(1)}, u32[]{:S(2)}, u32[]{:S(2)}) collective-permute-start(f32[80,128]{1,0:T(8,128)S(1)} %add.14), channel_id=1, source_target_pairs={{0,8},{1,9},{2,10},{3,11},{4,12},{5,13},{6,14},{7,15},{8,0},{9,1},... | collective-permute-start | bytes 122888 | tf_op jit(solution)/shard_map/ppermute | solution.py:177
  22.3 3.0 %collective-permute-start.6 = (f32[8,128]{1,0:T(8,128)S(1)}, f32[8,128]{1,0:T(8,128)S(1)}, u32[]{:S(2)}, u32[]{:S(2)}) collective-permute-start(f32[8,128]{1,0:T(8,128)S(1)} %get-tuple-element.9.refs_0_), channel_id=1, source_target_pairs={{0,17},{1,16},{2,19},{3,18},{4,21},{5,20},{6,23},{7,22},{8,25},{9,... | collective-permute-start | bytes 12296 | tf_op jit(solution)/shard_map/ppermute | solution.py:227
  22.3 3.6 %collective-permute-start.5 = (f32[8,128]{1,0:T(8,128)S(1)}, f32[8,128]{1,0:T(8,128)S(1)}, u32[]{:S(2)}, u32[]{:S(2)}) collective-permute-start(f32[8,128]{1,0:T(8,128)S(1)} %get-tuple-element.9.refs_0_), channel_id=1, source_target_pairs={{0,16},{16,0},{1,17},{17,1},{2,18},{18,2},{3,19},{19,3},{4,20},{20... | collective-permute-start | bytes 12296 | tf_op jit(solution)/shard_map/ppermute | solution.py:177
  24.1 1.8 %collective-permute-start.4 = (f32[8,128]{1,0:T(8,128)S(1)}, f32[8,128]{1,0:T(8,128)S(1)}, u32[]{:S(2)}, u32[]{:S(2)}) collective-permute-start(f32[8,128]{1,0:T(8,128)S(1)} %get-tuple-element.9.refs_0_), channel_id=1, source_target_pairs={{0,1},{1,0},{2,3},{3,2},{4,5},{5,4},{6,7},{7,6},{8,9},{9,8},{10,11... | collective-permute-start | bytes 12296 | tf_op jit(solution)/shard_map/ppermute | solution.py:177
